TPU v7x, 256 devices: a whole 4x4x8 slice. The times are simulated.
256 devices in a mesh: win: 4 (over x_hi, core), sta: 64 (over y, z, x_lo).
Axes of the slice: x: 4 (x_hi: 2, x_lo: 2; x = x_hi * 2 + x_lo), y: 4, z: 8, core: 2. Of those that a mesh axis runs over, the one named last changes fastest.
Arguments:
- samples: bfloat16 [256, 2097152], P('sta', 'win'), may hold values from -6 to 6
- coarse_taps: bfloat16 [16, 512], replicated, may hold values from -0.0625 to 0.0625
- fine_taps: bfloat16 [8, 64], replicated, may hold values from -0.25 to 0.25
Outputs:
- visibilities: bfloat16 [128, 64, 2, 256, 256], P('win', 'sta')
All inputs are finite; a program needn't handle non-finite values.
Results may differ from a plain program's by a relative error of at most 0.008.
Values may be sent and summed in bfloat16 or wider, within the bound.
A program may use at most 64 MiB of HBM per device.

v0:
```python
import math

import jax
import jax.numpy as jnp
from jax import lax
from jax.sharding import PartitionSpec as P

KEEP = 128


def from_behind(x, axis, by):
    size = lax.axis_size(axis)
    pairs = [(i, i + by) for i in range(size) if 0 <= i + by < size]
    return lax.ppermute(x, axis, pairs)


def coarse_matrix(frame_len, band_count):
    channels = frame_len // 8 + jnp.arange(band_count, dtype=jnp.int32)
    products = jnp.arange(frame_len, dtype=jnp.int32)[:, None] * channels[None, :]
    angles = (products % frame_len).astype(jnp.float32) * (2.0 * math.pi / frame_len)
    return jnp.concatenate([jnp.cos(angles), -jnp.sin(angles)], axis=1).astype(jnp.bfloat16)


def fine_tables(fine_len):
    products = (
        jnp.arange(fine_len, dtype=jnp.int32)[:, None]
        * jnp.arange(fine_len, dtype=jnp.int32)[None, :]
    )
    angles = (products % fine_len).astype(jnp.float32) * (2.0 * math.pi / fine_len)
    return (jnp.cos(angles), jnp.sin(angles))


def correlate(spectra_in, pieces):
    band_local, fine_local, sig_count, columns = spectra_in.shape
    split_view = spectra_in.reshape(
        band_local, fine_local, sig_count, pieces, 2, columns // (2 * pieces)
    )
    turned = jnp.stack([split_view[:, :, :, :, 1], -split_view[:, :, :, :, 0]], axis=4).reshape(
        band_local, fine_local, sig_count, columns
    )
    real_vis = jnp.einsum(
        "kqsc,kqtc->kqst", spectra_in, spectra_in, preferred_element_type=jnp.float32
    )
    imag_vis = jnp.einsum("kqsc,kqtc->kqst", turned, spectra_in, preferred_element_type=jnp.float32)
    return jnp.stack([real_vis, imag_vis], axis=2)


def per_device(samples, coarse_taps, fine_taps):
    sig_local, samp_local = samples.shape
    tap_count, frame_len = coarse_taps.shape
    fine_tap_count, fine_len = fine_taps.shape
    band_count = KEEP
    frame_count = samp_local // frame_len
    frames_local = samples.reshape(sig_local, frame_count, frame_len)
    earlier = from_behind(frames_local[:, frame_count - (tap_count - 1) :], "win", 1)
    padded = jnp.concatenate([earlier, frames_local], axis=1)
    windowed = jnp.zeros((sig_local, frame_count, frame_len), jnp.float32)
    for tap_index in range(tap_count):
        start = tap_count - 1 - tap_index
        windowed = windowed + coarse_taps[tap_index].astype(jnp.float32)[None, None, :] * padded[
            :, start : start + frame_count
        ].astype(jnp.float32)
    spectra = jnp.dot(
        windowed.astype(jnp.bfloat16).reshape(sig_local * frame_count, frame_len),
        coarse_matrix(frame_len, band_count),
        preferred_element_type=jnp.float32,
    )
    spectra = spectra.astype(jnp.bfloat16).reshape(sig_local, frame_count, 2 * band_count)
    history = (fine_tap_count - 1) * fine_len
    carried = from_behind(spectra[:, frame_count - history :], "win", 1)
    extended = jnp.concatenate([carried, spectra], axis=1)
    fine_count = frame_count // fine_len
    groups = extended.reshape(sig_local, fine_count + fine_tap_count - 1, fine_len, 2, band_count)
    filtered = jnp.zeros((sig_local, fine_count, fine_len, 2, band_count), jnp.float32)
    for tap_index in range(fine_tap_count):
        start = fine_tap_count - 1 - tap_index
        filtered = filtered + fine_taps[tap_index].astype(jnp.float32)[
            None, None, :, None, None
        ] * groups[:, start : start + fine_count].astype(jnp.float32)
    cosines, sines = fine_tables(fine_len)
    real_part = filtered[:, :, :, 0]
    imag_part = filtered[:, :, :, 1]
    highest = lax.Precision.HIGHEST
    out_real = jnp.einsum("qj,sgjk->kqsg", cosines, real_part, precision=highest) + jnp.einsum(
        "qj,sgjk->kqsg", sines, imag_part, precision=highest
    )
    out_imag = jnp.einsum("qj,sgjk->kqsg", cosines, imag_part, precision=highest) - jnp.einsum(
        "qj,sgjk->kqsg", sines, real_part, precision=highest
    )
    local_spectra = (
        jnp.stack([out_real, out_imag], axis=3)
        .astype(jnp.bfloat16)
        .reshape(band_count, fine_len, sig_local, 2 * fine_count)
    )
    frame_total = fine_count * lax.axis_size("win")
    moved = lax.all_to_all(local_spectra, "sta", split_axis=1, concat_axis=2, tiled=True)
    moved = lax.all_to_all(moved, "win", split_axis=0, concat_axis=3, tiled=True)
    vis_local = correlate(moved, lax.axis_size("win"))
    return (vis_local / frame_total).astype(jnp.bfloat16)


def solution(mesh):
    placed = (P("sta", "win"), P(), P())
    return jax.shard_map(
        per_device,
        mesh=mesh,
        in_specs=placed,
        out_specs=P("win", "sta", None, None, None),
        check_vma=False,
    )
```

profile of v0, /device:TPU:1, one launch (start us, length us, event | category | flops | bytes accessed | tf_op | source)
XLA Modules:
  0.0 184.8 jit_solution(17558840915557810946)
XLA Ops:
  0.0 3.0 %copy.46 = bf16[1,4,1024,512]{3,2,1,0:T(8,128)(2,1)S(1)} copy(bf16[1,4,1024,512]{3,1,2,0:T(4,128)(2,1)} %bitcast.112) | data formatting | bytes 8388608
  3.1 6.0 %collective-permute-start = (bf16[4,15,512]{2,1,0:T(8,128)(2,1)S(1)}, bf16[4,15,512]{2,1,0:T(8,128)(2,1)S(1)}, u32[]{:S(2)}, u32[]{:S(2)}) collective-permute-start(bf16[4,15,512]{2,1,0:T(8,128)(2,1)S(1)} %slice.212), channel_id=1, source_target_pairs={{0,64},{64,128},{128,192},{1,65},{65,129},{129,193},{2,66},{66,130... | collective-permute-start | bytes 184328 | tf_op jit(solution)/shard_map/ppermute | solution.py:14
  9.1 1.1 cosine_convert_fusion
  10.4 17.6 %add_convert_fusion = bf16[4,1024,512]{2,1,0:T(8,128)(2,1)S(1)} fusion(bf16[4,1024,512]{2,1,0:T(8,128)(2,1)S(1)} %bitcast.105, bf16[4,15,512]{2,1,0:T(8,128)(2,1)S(1)} %collective-permute-done, f32[512]{0:T(512)S(1)} %bitcast.128, f32[512]{0:T(512)S(1)} %bitcast.129, f32[512]{0:T(512)S(1)} %bitcast.115, f32[512]{0:T(512)S(1)} %bitcast.116, ...), kind=kLoop, calls=%fused_computation.16 | loop fusion | flops 195035136 | bytes 8482816 | tf_op jit(solution)/shard_map/convert_element_type | solution.py:64
  28.0 1.3 convolution_convert_fusion
  29.3 5.8 %collective-permute-start.1 = (bf16[4,448,256]{2,1,0:T(8,128)(2,1)S(1)}, bf16[4,448,256]{2,1,0:T(8,128)(2,1)S(1)}, u32[]{:S(2)}, u32[]{:S(2)}) collective-permute-start(bf16[4,448,256]{2,1,0:T(8,128)(2,1)S(1)} %slice.241), channel_id=1, source_target_pairs={{0,64},{64,128},{128,192},{1,65},{65,129},{129,193},{2,66},{66,130... | collective-permute-start | bytes 2752520 | tf_op jit(solution)/shard_map/ppermute | solution.py:14
  35.1 10.3 %collective-permute-done.1 = bf16[4,448,256]{2,1,0:T(8,128)(2,1)S(1)} collective-permute-done((bf16[4,448,256]{2,1,0:T(8,128)(2,1)S(1)}, bf16[4,448,256]{2,1,0:T(8,128)(2,1)S(1)}, u32[]{:S(2)}, u32[]{:S(2)}) %collective-permute-start.1) | collective-permute-done | bytes 917536 | tf_op jit(solution)/shard_map/ppermute | solution.py:14
  45.4 1.8 pad_maximum_fusion.1
  47.2 5.5 %reshape.257 = bf16[4,23,64,2,128]{4,3,2,1,0:T(2,128)(2,1)S(1)} reshape(bf16[4,1472,256]{2,1,0:T(8,128)(2,1)} %pad_maximum_fusion.1) | data formatting | bytes 6029312 | tf_op jit(solution)/shard_map/reshape | solution.py:73
  52.8 15.0 %fusion.63 = (bf16[4,16,64,2,128]{4,3,2,1,0:T(2,128)(2,1)S(1)}, bf16[4,16,64,2,128]{4,3,2,1,0:T(2,128)(2,1)S(1)}, bf16[4,16,64,2,128]{4,3,2,1,0:T(2,128)(2,1)S(1...) fusion(bf16[4,23,64,2,128]{4,3,2,1,0:T(2,128)(2,1)S(1)} %reshap, ...), kind=kLoop, calls=%fused_computation.126 | loop fusion | bytes 33554432 | tf_op jit(solution)/shard_map/slice | solution.py:79
  67.8 3.2 %multiply_add_fusion = f32[4,16,64,2,128]{4,2,1,0,3:T(8,128)S(1)} fusion(bf16[4,16,64,2,128]{4,3,2,1,0:T(2,128)(2,1)S(1)} %get-tuple-element.12, bf16[4,16,64,2,128]{4,3,2,1,0:T(2,128)(2,1)S(1)} %get-tuple-element.6, bf16[4,16,64,2,128]{4,3,2,1,0:T(2,128)(2,1)S(1)} %get-tuple-element.7, bf16[4,16,64,2,128]{4,3,2,1,0:T(2,128)(2,1)S(1)} %get-tuple-element.8, ...), kind=kLoop, calls=%fused_computation.38 | loop fusion | flops 24117248 | bytes 20973568 | tf_op jit(solution)/shard_map/add | solution.py:77
  71.0 2.1 %fusion.15 = f32[4,16,128,64]{2,3,1,0:T(8,128)S(1)} fusion(f32[4,16,64,2,128]{4,2,1,0,3:T(8,128)S(1)} %multiply_add_fusion), kind=kOutput, calls=%fused_computation.48 | convolution fusion | flops 402710528 | bytes 4194304 | tf_op jit(solution)/shard_map/qj,sgjk->kqsg/dot_general | solution.py:87
  73.1 2.1 %fusion.18 = f32[4,16,128,64]{2,3,1,0:T(8,128)S(1)} fusion(f32[4,16,64,2,128]{4,2,1,0,3:T(8,128)S(1)} %multiply_add_fusion), kind=kOutput, calls=%fused_computation.51 | convolution fusion | flops 402710528 | bytes 4194304 | tf_op jit(solution)/shard_map/qj,sgjk->kqsg/dot_general | solution.py:84
  75.3 2.3 %fusion.20 = bf16[128,64,4,1,16]{0,1,4,2,3:T(8,128)(2,1)S(1)} fusion(f32[4,16,128,64]{2,3,1,0:T(8,128)S(1)} %fusion.15, f32[4,16,64,2,128]{4,2,1,0,3:T(8,128)S(1)} %multiply_add_fusion), kind=kOutput, calls=%fused_computation.53 | convolution fusion | flops 403759104 | bytes 5242880 | tf_op jit(solution)/shard_map/qj,sgjk->kqsg/dot_general | solution.py:87
  77.6 2.3 %fusion.19 = bf16[128,64,4,1,16]{0,1,4,2,3:T(8,128)(2,1)S(1)} fusion(f32[4,16,128,64]{2,3,1,0:T(8,128)S(1)} %fusion.18, f32[4,16,64,2,128]{4,2,1,0,3:T(8,128)S(1)} %multiply_add_fusion), kind=kOutput, calls=%fused_computation.52 | convolution fusion | flops 403759104 | bytes 5242880 | tf_op jit(solution)/shard_map/qj,sgjk->kqsg/dot_general | solution.py:84
  80.1 1.6 copy.13
  81.7 52.7 %all_to_all.27 = bf16[128,64,4,32]{0,3,2,1:T(8,128)(2,1)S(1)} all-to-all(bf16[128,64,4,32]{0,3,2,1:T(8,128)(2,1)S(1)} %bitcast.106), channel_id=1, replica_groups=mesh['win'=4,'sta'=64] {'sta'}, dimensions={1} | all-to-all | bytes 4194304 | tf_op jit(solution)/shard_map/all_to_all | solution.py:96
  134.4 3.4 %copy.14 = bf16[128,1,256,32]{2,3,1,0:T(8,128)(2,1)} copy(bf16[128,1,256,32]{0,3,2,1:T(8,128)(2,1)S(1)} %bitcast.107) | data formatting | bytes 4194304 | tf_op jit(solution)/shard_map/all_to_all | solution.py:96
  137.9 31.6 %all_to_all.28 = bf16[128,1,256,32]{2,3,1,0:T(8,128)(2,1)S(1)} all-to-all(bf16[128,1,256,32]{2,3,1,0:T(8,128)(2,1)} %copy.14), channel_id=1, replica_groups=mesh['win'=4,'sta'=64] {'win'}, dimensions={0} | all-to-all | bytes 4194304 | tf_op jit(solution)/shard_map/all_to_all | solution.py:97
  169.5 0.2 copy.15
  169.8 1.3 convolution_bitcast_fusion.1
  171.3 1.3 convolution_bitcast_fusion
  172.6 4.4 %fusion = bf16[32,1,2,256,256]{4,3,0,2,1:T(8,128)(2,1)} fusion(f32[32,1,1,256,256]{4,3,0,2,1:T(8,128)S(1)} %convolution_bitcast_fusion, f32[32,1,1,256,256]{4,3,0,2,1:T(8,128)S(1)} %convolution_bitcast_fusion.1), kind=kLoop, calls=%fused_computation.15 | loop fusion | flops 12582912 | bytes 25165824 | tf_op jit(solution)/shard_map/convert_element_type | solution.py:99
  177.0 7.8 %copy.21 = bf16[32,1,2,256,256]{4,3,2,1,0:T(8,128)(2,1)} copy(bf16[32,1,2,256,256]{4,3,0,2,1:T(8,128)(2,1)} %fusion) | data formatting | bytes 16777216 | tf_op jit(solution)/shard_map/convert_element_type | solution.py:99
  (13 shorter events, 0.8 us)
Async XLA Ops:
  0.0 10.3 %copy-start = (bf16[16,512]{1,0:T(8,128)(2,1)S(1)}, bf16[16,512]{1,0:T(8,128)(2,1)}, u32[]{:S(2)}) copy-start(bf16[16,512]{1,0:T(8,128)(2,1)} %param.4) | copy-start | bytes 49156
  3.1 7.3 %collective-permute-start = (bf16[4,15,512]{2,1,0:T(8,128)(2,1)S(1)}, bf16[4,15,512]{2,1,0:T(8,128)(2,1)S(1)}, u32[]{:S(2)}, u32[]{:S(2)}) collective-permute-start(bf16[4,15,512]{2,1,0:T(8,128)(2,1)S(1)} %slice.212), channel_id=1, source_target_pairs={{0,64},{64,128},{128,192},{1,65},{65,129},{129,193},{2,66},{66,130... | collective-permute-start | bytes 184328 | tf_op jit(solution)/shard_map/ppermute | solution.py:14
  28.0 7.1 %copy-start.1 = (bf16[8,64]{1,0:T(8,128)(2,1)S(1)}, bf16[8,64]{1,0:T(8,128)(2,1)}, u32[]{:S(2)}) copy-start(bf16[8,64]{1,0:T(8,128)(2,1)} %param.5) | copy-start | bytes 3076
  29.3 16.1 %collective-permute-start.1 = (bf16[4,448,256]{2,1,0:T(8,128)(2,1)S(1)}, bf16[4,448,256]{2,1,0:T(8,128)(2,1)S(1)}, u32[]{:S(2)}, u32[]{:S(2)}) collective-permute-start(bf16[4,448,256]{2,1,0:T(8,128)(2,1)S(1)} %slice.241), channel_id=1, source_target_pairs={{0,64},{64,128},{128,192},{1,65},{65,129},{129,193},{2,66},{66,130... | collective-permute-start | bytes 2752520 | tf_op jit(solution)/shard_map/ppermute | solution.py:14
where the time goes:
time: 185 us
  blocking collectives  84.3 us (46%)
  local copies, waits for them, and re-layouts  36.6 us (20%)
  other arithmetic  28.6 us (15%)
  matrix products  12.8 us (7%)
  starting transfers between devices  11.8 us (6%)
  waiting for transfers between devices  10.4 us (6%)
    all_to_all x1, blocking collectives, per_device(): lax.all_to_all(local_spectra, 'sta', split_axis=1, concat_axis=2, tiled=T...  52.7 us
    all_to_all x1, blocking collectives, per_device(): lax.all_to_all(moved, 'win', split_axis=0, concat_axis=3, tiled=True)  31.6 us
    convert_element_type x1, other arithmetic, per_device(): windowed.astype(jnp.bfloat16).reshape(sig_local * frame_count, frame_len)  17.6 us
    slice x1, local copies, waits for them, and re-layouts, per_device(): groups[:, start:start + fine_count].astype(jnp.float32)  15 us
    ppermute x2, starting transfers between devices, from_behind(): return lax.ppermute(x, axis, pairs)  11.8 us
    ppermute x2, waiting for transfers between devices, from_behind(): return lax.ppermute(x, axis, pairs)  10.4 us
    convert_element_type x1, local copies, waits for them, and re-layouts, per_device(): return (vis_local / frame_total).astype(jnp.bfloat16)  7.77 us
    reshape x1, local copies, waits for them, and re-layouts, per_device(): extended.reshape(sig_local, fine_count + fine_tap_count - 1, fine_len, 2,...  5.53 us
  transfers between devices with their start and end apart: 2, of which 2 were waited for; matrix products, arithmetic and copies ran while one was open for 1% of the time, Pallas kernels for 0%

commit v1 on v0

--- a/solution.py
+++ b/solution.py
@@ -3,9 +3,12 @@
 import jax
 import jax.numpy as jnp
 from jax import lax
+from jax.experimental import pallas as pl
+from jax.experimental.pallas import tpu as pltpu
 from jax.sharding import PartitionSpec as P
 
 KEEP = 128
+MESH_ID = pl.DeviceIdType.MESH
 
 
 def from_behind(x, axis, by):
@@ -30,19 +33,72 @@
     return (jnp.cos(angles), jnp.sin(angles))
 
 
+def exchange_kernel(n_win, n_sta, send_ref, recv_ref, local_sem, send_sem, recv_sem):
+    n_all = n_win * n_sta
+    my_win = lax.axis_index("win")
+    my_sta = lax.axis_index("sta")
+    me = my_win * n_sta + my_sta
+    barrier = pltpu.get_barrier_semaphore()
+
+    def peer(step):
+        other = lax.rem(me + step, n_all)
+        return other, (other // n_sta, lax.rem(other, n_sta))
+
+    def greet(step, carry):
+        _, where = peer(step)
+        pl.semaphore_signal(barrier, inc=1, device_id=where, device_id_type=MESH_ID)
+        return carry
+
+    lax.fori_loop(1, n_all, greet, 0)
+    own = pltpu.make_async_copy(send_ref.at[me], recv_ref.at[me], local_sem)
+    own.start()
+    pl.semaphore_wait(barrier, n_all - 1)
+
+    def post(step, carry):
+        other, where = peer(step)
+        pltpu.make_async_remote_copy(
+            src_ref=send_ref.at[other],
+            dst_ref=recv_ref.at[me],
+            send_sem=send_sem,
+            recv_sem=recv_sem,
+            device_id=where,
+            device_id_type=MESH_ID,
+        ).start()
+        return carry
+
+    lax.fori_loop(1, n_all, post, 0)
+    own.wait()
+    most = recv_ref.at[pl.ds(0, n_all - 1)]
+    pltpu.make_async_copy(most, most, recv_sem).wait()
+    pltpu.make_async_copy(most, most, send_sem).wait()
+
+
+def exchange(blocks):
+    n_win, n_sta = lax.axis_size("win"), lax.axis_size("sta")
+
+    def kernel(*refs):
+        exchange_kernel(n_win, n_sta, *refs)
+
+    return pl.pallas_call(
+        kernel,
+        out_shape=jax.ShapeDtypeStruct(blocks.shape, blocks.dtype),
+        in_specs=[pl.BlockSpec(memory_space=pltpu.VMEM)],
+        out_specs=pl.BlockSpec(memory_space=pltpu.VMEM),
+        scratch_shapes=[pltpu.SemaphoreType.DMA] * 3,
+        compiler_params=pltpu.CompilerParams(collective_id=0, has_side_effects=True),
+        name="exchange",
+    )(blocks)
+
+
 def correlate(spectra_in, pieces):
-    band_local, fine_local, sig_count, columns = spectra_in.shape
-    split_view = spectra_in.reshape(
-        band_local, fine_local, sig_count, pieces, 2, columns // (2 * pieces)
+    band_local, sig_count, columns = spectra_in.shape
+    split_view = spectra_in.reshape(band_local, sig_count, pieces, 2, columns // (2 * pieces))
+    turned = jnp.stack([split_view[:, :, :, 1], -split_view[:, :, :, 0]], axis=3).reshape(
+        band_local, sig_count, columns
     )
-    turned = jnp.stack([split_view[:, :, :, :, 1], -split_view[:, :, :, :, 0]], axis=4).reshape(
-        band_local, fine_local, sig_count, columns
-    )
-    real_vis = jnp.einsum(
-        "kqsc,kqtc->kqst", spectra_in, spectra_in, preferred_element_type=jnp.float32
-    )
-    imag_vis = jnp.einsum("kqsc,kqtc->kqst", turned, spectra_in, preferred_element_type=jnp.float32)
-    return jnp.stack([real_vis, imag_vis], axis=2)
+    real_vis = jnp.einsum("ksc,ktc->kst", spectra_in, spectra_in, preferred_element_type=jnp.float32)
+    imag_vis = jnp.einsum("ksc,ktc->kst", turned, spectra_in, preferred_element_type=jnp.float32)
+    return jnp.stack([real_vis, imag_vis], axis=1)[:, None]
 
 
 def per_device(samples, coarse_taps, fine_taps):
@@ -50,6 +106,7 @@
     tap_count, frame_len = coarse_taps.shape
     fine_tap_count, fine_len = fine_taps.shape
     band_count = KEEP
+    n_win, n_sta = lax.axis_size("win"), lax.axis_size("sta")
     frame_count = samp_local // frame_len
     frames_local = samples.reshape(sig_local, frame_count, frame_len)
     earlier = from_behind(frames_local[:, frame_count - (tap_count - 1) :], "win", 1)
@@ -87,16 +144,20 @@
     out_imag = jnp.einsum("qj,sgjk->kqsg", cosines, imag_part, precision=highest) - jnp.einsum(
         "qj,sgjk->kqsg", sines, real_part, precision=highest
     )
+    band_local = band_count // n_win
+    block_lanes = sig_local * 2 * fine_count
     local_spectra = (
         jnp.stack([out_real, out_imag], axis=3)
         .astype(jnp.bfloat16)
-        .reshape(band_count, fine_len, sig_local, 2 * fine_count)
+        .reshape(n_win, band_local, n_sta, block_lanes)
     )
-    frame_total = fine_count * lax.axis_size("win")
-    moved = lax.all_to_all(local_spectra, "sta", split_axis=1, concat_axis=2, tiled=True)
-    moved = lax.all_to_all(moved, "win", split_axis=0, concat_axis=3, tiled=True)
-    vis_local = correlate(moved, lax.axis_size("win"))
-    return (vis_local / frame_total).astype(jnp.bfloat16)
+    blocks = jnp.transpose(local_spectra, (0, 2, 1, 3)).reshape(n_win * n_sta, band_local, block_lanes)
+    moved = exchange(blocks).reshape(n_win, n_sta, band_local, sig_local, 2 * fine_count)
+    moved = jnp.transpose(moved, (2, 1, 3, 0, 4)).reshape(
+        band_local, n_sta * sig_local, n_win * 2 * fine_count
+    )
+    frame_total = fine_count * n_win
+    return (correlate(moved, n_win) / frame_total).astype(jnp.bfloat16)
 
 
 def solution(mesh):

time: 185 us -> 242 us (1.31)
  blocking collectives: 84.3 us -> 0 us
  local copies, waits for them, and re-layouts: 36.6 us -> 110 us
  Pallas kernels: 0 us -> 64.7 us
    all_to_all x2 -> x0, blocking collectives: 84.3 us -> none  [the longest x1 52.7 us: per_device(): lax.all_to_all(local_spectra, 'sta', split_axis=1, concat_axis=2, tiled=T...]
    pallas_call x0 -> x1, Pallas kernels: none -> 64.7 us  [exchange(): pl.pallas_call(kernel, out_shape=jax.ShapeDtypeStruct(blocks.shape, block...]
    transpose x0 -> x3, local copies, waits for them, and re-layouts: none -> 37.9 us  [the longest x2 32.3 us: per_device(): jnp.transpose(moved, (2, 1, 3, 0, 4))]
    reshape x0 -> x2, local copies, waits for them, and re-layouts: none -> 12.8 us  [the longest x1 9.5 us: per_device(): jnp.transpose(moved, (2, 1, 3, 0, 4))]
    slice x0 -> x2, local copies, waits for them, and re-layouts: none -> 12.6 us  [correlate(): split_view[:, :, :, 1]]
    unnamed x5 -> x8, local copies, waits for them, and re-layouts: 3.05 us -> 9.2 us
    another operation x1, local copies, waits for them, and re-layouts: 1.57 us -> 6.62 us  [per_device(): jnp.stack([out_real, out_imag], axis=3).astype(jnp.bfloat16)]
    all_to_all x2 -> x0, local copies, waits for them, and re-layouts: 3.65 us -> none  [the longest x1 3.44 us: per_device(): lax.all_to_all(local_spectra, 'sta', split_axis=1, concat_axis=2, tiled=T...]
  transfers between devices with their start and end apart: 2 -> 2, of which waited for: 2 -> 2; matrix products, arithmetic and copies ran while one was open for 1% -> 0% of each run, Pallas kernels for 0% -> 0%
where the time goes in v1:
time: 242 us; the launch traced here: 240 us
  local copies, waits for them, and re-layouts  110 us (45%)
  Pallas kernels  64.7 us (27%)
  other arithmetic  29.7 us (12%)
  matrix products  12.7 us (5%)
  starting transfers between devices  11.8 us (5%)
  waiting for transfers between devices  10.4 us (4%)
    pallas_call x1, Pallas kernels, exchange(): pl.pallas_call(kernel, out_shape=jax.ShapeDtypeStruct(blocks.shape, block...  64.7 us
    transpose x2, local copies, waits for them, and re-layouts, per_device(): jnp.transpose(moved, (2, 1, 3, 0, 4))  32.3 us
    convert_element_type x1, other arithmetic, per_device(): windowed.astype(jnp.bfloat16).reshape(sig_local * frame_count, frame_len)  17.6 us
    slice x1, local copies, waits for them, and re-layouts, per_device(): groups[:, start:start + fine_count].astype(jnp.float32)  15 us
    slice x2, local copies, waits for them, and re-layouts, correlate(): split_view[:, :, :, 1]  12.6 us
    ppermute x2, starting transfers between devices, from_behind(): return lax.ppermute(x, axis, pairs)  11.8 us
    ppermute x2, waiting for transfers between devices, from_behind(): return lax.ppermute(x, axis, pairs)  10.4 us
    reshape x1, local copies, waits for them, and re-layouts, per_device(): jnp.transpose(moved, (2, 1, 3, 0, 4))  9.5 us
  transfers between devices with their start and end apart: 2, of which 2 were waited for; matrix products, arithmetic and copies ran while one was open for 0% of the time, Pallas kernels for 0%

profile of v1, /device:TPU:1, one launch (start us, length us, event | category | flops | bytes accessed | tf_op | source)
XLA Modules:
  0.0 240.0 jit_solution(12801987335766732835)
XLA Ops:
  0.0 3.0 %copy.78 = bf16[1,4,1024,512]{3,2,1,0:T(8,128)(2,1)S(1)} copy(bf16[1,4,1024,512]{3,1,2,0:T(4,128)(2,1)} %bitcast.112) | data formatting | bytes 8388608
  3.1 6.0 %collective-permute-start = (bf16[4,15,512]{2,1,0:T(8,128)(2,1)S(1)}, bf16[4,15,512]{2,1,0:T(8,128)(2,1)S(1)}, u32[]{:S(2)}, u32[]{:S(2)}) collective-permute-start(bf16[4,15,512]{2,1,0:T(8,128)(2,1)S(1)} %slice.212), channel_id=1, source_target_pairs={{0,64},{64,128},{128,192},{1,65},{65,129},{129,193},{2,66},{66,130... | collective-permute-start | bytes 184328 | tf_op jit(solution)/shard_map/ppermute | solution.py:17
  10.4 17.6 %add_convert_fusion = bf16[4,1024,512]{2,1,0:T(8,128)(2,1)S(1)} fusion(bf16[4,1024,512]{2,1,0:T(8,128)(2,1)S(1)} %bitcast.106, bf16[4,15,512]{2,1,0:T(8,128)(2,1)S(1)} %collective-permute-done, f32[512]{0:T(512)S(1)} %bitcast.128, f32[512]{0:T(512)S(1)} %bitcast.129, f32[512]{0:T(512)S(1)} %bitcast.115, f32[512]{0:T(512)S(1)} %bitcast.116, ...), kind=kLoop, calls=%fused_computation.16 | loop fusion | flops 195035136 | bytes 8482816 | tf_op jit(solution)/shard_map/convert_element_type | solution.py:121
  29.3 5.8 %collective-permute-start.1 = (bf16[4,448,256]{2,1,0:T(8,128)(2,1)S(1)}, bf16[4,448,256]{2,1,0:T(8,128)(2,1)S(1)}, u32[]{:S(2)}, u32[]{:S(2)}) collective-permute-start(bf16[4,448,256]{2,1,0:T(8,128)(2,1)S(1)} %slice.241), channel_id=1, source_target_pairs={{0,64},{64,128},{128,192},{1,65},{65,129},{129,193},{2,66},{66,130... | collective-permute-start | bytes 2752520 | tf_op jit(solution)/shard_map/ppermute | solution.py:17
  35.1 10.3 %collective-permute-done.1 = bf16[4,448,256]{2,1,0:T(8,128)(2,1)S(1)} collective-permute-done((bf16[4,448,256]{2,1,0:T(8,128)(2,1)S(1)}, bf16[4,448,256]{2,1,0:T(8,128)(2,1)S(1)}, u32[]{:S(2)}, u32[]{:S(2)}) %collective-permute-start.1) | collective-permute-done | bytes 917536 | tf_op jit(solution)/shard_map/ppermute | solution.py:17
  47.2 5.5 %reshape.238 = bf16[4,23,64,2,128]{4,3,2,1,0:T(2,128)(2,1)S(1)} reshape(bf16[4,1472,256]{2,1,0:T(8,128)(2,1)} %pad_maximum_fusion.1) | data formatting | bytes 6029312 | tf_op jit(solution)/shard_map/reshape | solution.py:130
  52.8 15.0 %fusion.64 = (bf16[4,16,64,2,128]{4,3,2,1,0:T(2,128)(2,1)S(1)}, bf16[4,16,64,2,128]{4,3,2,1,0:T(2,128)(2,1)S(1)}, bf16[4,16,64,2,128]{4,3,2,1,0:T(2,128)(2,1)S(1...) fusion(bf16[4,23,64,2,128]{4,3,2,1,0:T(2,128)(2,1)S(1)} %reshap, ...), kind=kLoop, calls=%fused_computation.126 | loop fusion | bytes 33554432 | tf_op jit(solution)/shard_map/slice | solution.py:136
  67.8 3.2 %multiply_add_fusion = f32[4,16,64,2,128]{4,2,1,0,3:T(8,128)S(1)} fusion(bf16[4,16,64,2,128]{4,3,2,1,0:T(2,128)(2,1)S(1)} %get-tuple-element.14, bf16[4,16,64,2,128]{4,3,2,1,0:T(2,128)(2,1)S(1)} %get-tuple-element.8, bf16[4,16,64,2,128]{4,3,2,1,0:T(2,128)(2,1)S(1)} %get-tuple-element.9, bf16[4,16,64,2,128]{4,3,2,1,0:T(2,128)(2,1)S(1)} %get-tuple-element.10, ...), kind=kLoop, calls=%fused_computation.38 | loop fusion | flops 24117248 | bytes 20973568 | tf_op jit(solution)/shard_map/add | solution.py:134
  71.0 2.1 fusion.15
  75.3 2.3 fusion.20
  77.6 2.3 fusion.19
  80.1 6.6 %copy.47 = bf16[128,64,4,2,16]{1,4,3,2,0:T(8,128)(2,1)} copy(bf16[128,64,4,2,16]{0,1,4,2,3:T(8,128)(2,1)S(1)} %pad_maximum_fusion.2) | data formatting | bytes 4194304 | tf_op jit(solution)/shard_map/stack | solution.py:150
  86.7 5.6 %copy.48 = bf16[4,64,32,128]{3,2,1,0:T(8,128)(2,1)} copy(bf16[4,64,32,128]{1,3,2,0:T(8,128)(2,1)} %bitcast.107) | data formatting | bytes 4194304 | tf_op jit(solution)/shard_map/transpose | solution.py:154
  92.3 64.7 %exchange.1 = bf16[256,32,128]{2,1,0:T(8,128)(2,1)} custom-call(bf16[256,32,128]{2,1,0:T(8,128)(2,1)} %bitcast.108), custom_call_target="tpu_custom_call" | custom-call | tf_op jit(solution)/shard_map/exchange/pallas_call | solution.py:82
  157.1 3.0 %copy.49 = bf16[256,32,128]{0,2,1:T(8,128)(2,1)S(1)} copy(bf16[256,32,128]{2,1,0:T(8,128)(2,1)} %exchange.1) | data formatting | bytes 4194304 | tf_op jit(solution)/shard_map/exchange/pallas_call | solution.py:82
  160.1 3.3 %reshape.240 = bf16[4,64,32,4,32]{1,0,4,3,2:T(4,128)(2,1)} reshape(bf16[256,32,128]{0,2,1:T(8,128)(2,1)S(1)} %copy.49) | data formatting | bytes 4194304 | tf_op jit(solution)/shard_map/reshape | solution.py:155
  163.4 17.9 %copy.51 = bf16[32,64,4,4,32]{0,4,3,2,1:T(8,128)(2,1)} copy(bf16[32,64,4,4,32]{1,3,4,2,0:T(4,128)(2,1)} %bitcast.102) | data formatting | bytes 4194304 | tf_op jit(solution)/shard_map/transpose | solution.py:156
  181.3 14.3 %copy.50 = bf16[32,64,4,4,32]{4,3,2,1,0:T(4,128)(2,1)} copy(bf16[32,64,4,4,32]{1,3,4,2,0:T(4,128)(2,1)} %bitcast.103) | data formatting | bytes 4194304 | tf_op jit(solution)/shard_map/transpose | solution.py:156
  195.6 6.4 %fusion.63 = (bf16[32,256,4,1,16]{0,4,3,2,1:T(8,128)(2,1)}, bf16[32,256,4,1,16]{0,4,3,2,1:T(8,128)(2,1)}) fusion(bf16[32,256,4,2,16]{0,4,3,2,1:T(8,128)(2,1)} %bitcast.104), kind=kLoop, calls=%fused_computation.125 | loop fusion | bytes 4194304 | tf_op jit(solution)/shard_map/slice | solution.py:96
  202.1 6.1 %copy.53 = bf16[32,256,4,1,16]{1,4,3,2,0:T(8,128)(2,1)S(1)} copy(bf16[32,256,4,1,16]{0,4,3,2,1:T(8,128)(2,1)} %get-tuple-element.5) | data formatting | bytes 2097152 | tf_op jit(solution)/shard_map/slice | solution.py:96
  208.2 6.2 %copy.67 = bf16[32,256,4,1,16]{1,4,3,2,0:T(8,128)(2,1)S(1)} copy(bf16[32,256,4,1,16]{0,4,3,2,1:T(8,128)(2,1)} %get-tuple-element.6) | data formatting | bytes 2097152
  215.6 9.5 %reshape.241 = bf16[32,256,128]{2,1,0:T(8,128)(2,1)S(1)} reshape(bf16[32,64,4,4,32]{4,3,2,1,0:T(4,128)(2,1)} %copy.50) | data formatting | bytes 4194304 | tf_op jit(solution)/shard_map/reshape | solution.py:156
  227.9 4.4 %fusion = bf16[32,1,2,256,256]{4,3,0,2,1:T(8,128)(2,1)} fusion(f32[32,1,1,256,256]{4,3,0,2,1:T(8,128)S(1)} %convolution_bitcast_fusion, f32[32,1,1,256,256]{4,3,0,2,1:T(8,128)S(1)} %convolution_bitcast_fusion.1), kind=kLoop, calls=%fused_computation.15 | loop fusion | flops 12582912 | bytes 25165824 | tf_op jit(solution)/shard_map/convert_element_type | solution.py:160
  232.3 7.8 %copy.55 = bf16[32,1,2,256,256]{4,3,2,1,0:T(8,128)(2,1)} copy(bf16[32,1,2,256,256]{4,3,0,2,1:T(8,128)(2,1)} %fusion) | data formatting | bytes 16777216 | tf_op jit(solution)/shard_map/convert_element_type | solution.py:160
  (21 shorter events, 10.8 us)
Async XLA Ops:
  0.0 10.3 %copy-start.1 = (bf16[16,512]{1,0:T(8,128)(2,1)S(1)}, bf16[16,512]{1,0:T(8,128)(2,1)}, u32[]{:S(2)}) copy-start(bf16[16,512]{1,0:T(8,128)(2,1)} %param.4) | copy-start | bytes 49156
  3.1 7.3 %collective-permute-start = (bf16[4,15,512]{2,1,0:T(8,128)(2,1)S(1)}, bf16[4,15,512]{2,1,0:T(8,128)(2,1)S(1)}, u32[]{:S(2)}, u32[]{:S(2)}) collective-permute-start(bf16[4,15,512]{2,1,0:T(8,128)(2,1)S(1)} %slice.212), channel_id=1, source_target_pairs={{0,64},{64,128},{128,192},{1,65},{65,129},{129,193},{2,66},{66,130... | collective-permute-start | bytes 184328 | tf_op jit(solution)/shard_map/ppermute | solution.py:17
  28.0 7.1 %copy-start.2 = (bf16[8,64]{1,0:T(8,128)(2,1)S(1)}, bf16[8,64]{1,0:T(8,128)(2,1)}, u32[]{:S(2)}) copy-start(bf16[8,64]{1,0:T(8,128)(2,1)} %param.5) | copy-start | bytes 3076
  29.3 16.1 %collective-permute-start.1 = (bf16[4,448,256]{2,1,0:T(8,128)(2,1)S(1)}, bf16[4,448,256]{2,1,0:T(8,128)(2,1)S(1)}, u32[]{:S(2)}, u32[]{:S(2)}) collective-permute-start(bf16[4,448,256]{2,1,0:T(8,128)(2,1)S(1)} %slice.241), channel_id=1, source_target_pairs={{0,64},{64,128},{128,192},{1,65},{65,129},{129,193},{2,66},{66,130... | collective-permute-start | bytes 2752520 | tf_op jit(solution)/shard_map/ppermute | solution.py:17
  225.1 1.3 copy-start

commit v2 on v0

v2 whole, which is shorter than its diff:
```python
import math

import jax
import jax.numpy as jnp
import numpy as np
from jax import lax
from jax.experimental import pallas as pl
from jax.experimental.pallas import tpu as pltpu
from jax.sharding import PartitionSpec as P

KEEP = 128
QUAD = 4
MESH_ID = pl.DeviceIdType.MESH
NT_DIMS = (((1,), (1,)), ((), ()))


def coarse_matrix(frame_len, band_count):
    channels = frame_len // 8 + np.arange(band_count)
    angles = (np.arange(frame_len)[:, None] * channels[None, :]) % frame_len
    angles = angles.astype(np.float32) * np.float32(2.0 * math.pi / frame_len)
    return np.concatenate([np.cos(angles), -np.sin(angles)], axis=1).astype(jnp.bfloat16)


def fine_matrix(fine_len):
    angles = (np.arange(fine_len)[:, None] * np.arange(fine_len)[None, :]) % fine_len
    angles = angles.astype(np.float32) * np.float32(2.0 * math.pi / fine_len)
    cosines, sines = np.cos(angles), np.sin(angles)
    real_rows = np.concatenate([cosines, sines], axis=1)
    imag_rows = np.concatenate([-sines, cosines], axis=1)
    both = np.stack([real_rows, imag_rows], axis=1)
    return np.repeat(both.reshape(2 * fine_len, 2 * fine_len), QUAD, axis=0).astype(np.float32)


def pick_matrix(channels, senders, lanes):
    row = np.arange(channels * senders)
    col = np.arange(senders * lanes)
    same_sender = (row % senders)[:, None] == (col // lanes)[None, :]
    same_channel = (row // senders)[:, None] == (col % channels)[None, :]
    return (same_sender & same_channel).astype(jnp.bfloat16)


def make_channeliser(n_win, n_sta, sig_count, frame_count, tap_count, frame_len, fine_tap_count, fine_len):
    n_all = n_win * n_sta
    cols = frame_len // 128
    halo_rows = 16
    block = 128
    n_blocks = frame_count // block
    fine_count = frame_count // fine_len
    frame_rows = 2 * fine_len
    old_rows = (fine_tap_count - 1) * frame_rows
    span = fine_tap_count - 1 + QUAD
    n_quads = fine_count // QUAD
    band_local = KEEP // n_win
    group = 8
    n_groups = n_sta // group

    def kernel(
        x_ref, coarse_ref, fine_ref, dft_ref, table_ref, pick_ref, out_ref,
        wide, edge, spec, banded, stage, outbox, inbox,
        own_sem, edge_send, edge_recv, old_send, old_recv, send_sem, recv_sem,
    ):
        my_win = lax.axis_index("win")
        my_sta = lax.axis_index("sta")
        barrier = pltpu.get_barrier_semaphore()

        def peer(step):
            win = lax.rem(my_win + step // n_sta, n_win)
            sta = lax.rem(my_sta + lax.rem(step, n_sta), n_sta)
            return win, sta

        def greet(step, carry):
            pl.semaphore_signal(barrier, inc=1, device_id=peer(step), device_id_type=MESH_ID)
            return carry

        lax.fori_loop(1, n_all, greet, 0)

        def edge_copy(sig):
            return pltpu.make_async_remote_copy(
                src_ref=x_ref.at[sig, pl.ds(frame_count - halo_rows, halo_rows)],
                dst_ref=edge.at[sig],
                send_sem=edge_send.at[sig],
                recv_sem=edge_recv.at[sig],
                device_id=(my_win + 1, my_sta),
                device_id_type=MESH_ID,
            )

        def old_copy(sig):
            return pltpu.make_async_remote_copy(
                src_ref=spec.at[sig, pl.ds(fine_count * frame_rows, old_rows)],
                dst_ref=spec.at[sig, pl.ds(0, old_rows)],
                send_sem=old_send.at[sig],
                recv_sem=old_recv.at[sig],
                device_id=(my_win + 1, my_sta),
                device_id_type=MESH_ID,
            )

        def build_banded():
            taps = fine_ref[...].astype(jnp.float32)
            taps = jnp.concatenate([taps, taps], axis=1)
            place = lax.rem(lax.broadcasted_iota(jnp.int32, (2 * QUAD, frame_rows), 0), QUAD)
            for d in range(span):
                weights = jnp.zeros((2 * QUAD, frame_rows), jnp.float32)
                for gl in range(QUAD):
                    m = gl + fine_tap_count - 1 - d
                    if 0 <= m < fine_tap_count:
                        row = jnp.broadcast_to(taps[m : m + 1], weights.shape)
                        weights = jnp.where(place == gl, row, weights)
                table = table_ref[...].reshape(fine_len, 2 * QUAD, frame_rows)
                part = (table * weights[None]).reshape(fine_len * 2 * QUAD, frame_rows)
                banded[:, d * frame_rows : (d + 1) * frame_rows] = part.astype(jnp.bfloat16)

        def widen(sig):
            for k in range(cols):
                wide[k, pl.ds(halo_rows, frame_count)] = x_ref[
                    sig, :, pl.ds(k * 128, 128)
                ].astype(jnp.float32)

        def coarse_block(sig, i):
            pieces = []
            for k in range(cols):
                total = jnp.zeros((block, 128), jnp.float32)
                for m in range(tap_count):
                    row = coarse_ref[m : m + 1, k * 128 : (k + 1) * 128].astype(jnp.float32)
                    total = total + row * wide[k, pl.ds(i * block + halo_rows - m, block)]
                pieces.append(total.astype(jnp.bfloat16))
            windowed = jnp.concatenate(pieces, axis=1)
            result = jnp.dot(windowed, dft_ref[...], preferred_element_type=jnp.float32)
            result = result.astype(jnp.bfloat16)
            base = pl.multiple_of(old_rows + i * (block // fine_len) * frame_rows, frame_rows)
            for h in range(block // fine_len):
                for p in range(2):
                    spec[sig, pl.ds(base + (2 * h + p) * fine_len, fine_len)] = result[
                        h * fine_len : (h + 1) * fine_len, p * KEEP : (p + 1) * KEEP
                    ]

        def coarse(sig, first):
            widen(sig)

            def step(i, carry):
                coarse_block(sig, i)
                return carry

            lax.fori_loop(n_blocks // 2, n_blocks, step, 0)
            if first:
                pl.semaphore_wait(barrier, n_all - 1)

                @pl.when(my_win < n_win - 1)
                def _():
                    for s in range(sig_count):
                        edge_copy(s).start()

            @pl.when(my_win < n_win - 1)
            def _():
                old_copy(sig).start()

            lax.fori_loop(1, n_blocks // 2, step, 0)

            @pl.when(my_win > 0)
            def _():
                edge_copy(sig).wait_recv()
                for k in range(cols):
                    wide[k, pl.ds(0, halo_rows)] = edge[sig, :, pl.ds(k * 128, 128)].astype(
                        jnp.float32
                    )

            @pl.when(my_win == 0)
            def _():
                for k in range(cols):
                    wide[k, pl.ds(0, halo_rows)] = jnp.zeros((halo_rows, 128), jnp.float32)
                spec[sig, pl.ds(0, old_rows)] = jnp.zeros((old_rows, KEEP), jnp.bfloat16)

            coarse_block(sig, 0)

        lane = lax.broadcasted_iota(jnp.int32, (64, 128), 1)

        def fine(sig):
            @pl.when(my_win > 0)
            def _():
                old_copy(sig).wait_recv()

            for quad in range(n_quads):
                stage[quad] = jnp.dot(
                    banded[...],
                    spec[sig, pl.ds(quad * QUAD * frame_rows, span * frame_rows)],
                    preferred_element_type=jnp.float32,
                )

            def turn(i, carry):
                rows = pl.ds(pl.multiple_of(i * 64, 64), 64)
                a, b, c, d = [stage[quad, rows] for quad in range(4)]
                low = lane < 64
                a, c = (
                    jnp.where(low, a, pltpu.roll(c, 64, 1)),
                    jnp.where(low, pltpu.roll(a, 64, 1), c),
                )
                b, d = (
                    jnp.where(low, b, pltpu.roll(d, 64, 1)),
                    jnp.where(low, pltpu.roll(b, 64, 1), d),
                )
                even = lax.rem(lane, 64) < 32
                a, b = (
                    jnp.where(even, a, pltpu.roll(b, 32, 1)),
                    jnp.where(even, pltpu.roll(a, 96, 1), b),
                )
                c, d = (
                    jnp.where(even, c, pltpu.roll(d, 32, 1)),
                    jnp.where(even, pltpu.roll(c, 96, 1), d),
                )
                for win, value in enumerate((a, b, c, d)):
                    outbox[sig, pl.ds(win * n_sta + i * 8, 8)] = value.reshape(8, 8, 128).astype(jnp.bfloat16)
                return carry

            lax.fori_loop(0, fine_len // 8, turn, 0)

        def post(sig):
            mine = inbox.at[
                sig,
                my_sta // group,
                my_win,
                :,
                pl.ds(pl.multiple_of(lax.rem(my_sta, group) * 128, 128), 128),
            ]
            pltpu.make_async_copy(outbox.at[sig, my_win * n_sta + my_sta], mine, own_sem.at[sig]).start()

            def send(step, carry):
                win, sta = peer(step)
                pltpu.make_async_remote_copy(
                    src_ref=outbox.at[sig, win * n_sta + sta],
                    dst_ref=mine,
                    send_sem=send_sem.at[sig],
                    recv_sem=recv_sem.at[sig],
                    device_id=(win, sta),
                    device_id_type=MESH_ID,
                ).start()
                return carry

            lax.fori_loop(1, n_all, send, 0)

        def all_but_one(sig, sem):
            most = outbox.at[sig, pl.ds(0, n_all - 1)]
            pltpu.make_async_copy(most, most, sem).wait()

        def collect(sig):
            all_but_one(sig, recv_sem.at[sig])
            first = outbox.at[sig, 0]
            pltpu.make_async_copy(first, first, own_sem.at[sig]).wait()
            which = lax.rem(lax.broadcasted_iota(jnp.int32, (8 * n_win, group * 128), 1), 128) // 32

            def turn(i, carry):
                got = inbox[sig, i].astype(jnp.float32).reshape(n_win * 8, group * 128)
                spread = jnp.concatenate(
                    [
                        jnp.where(which == quad, got, 0.0).astype(jnp.bfloat16)
                        for quad in range(n_quads)
                    ],
                    axis=0,
                )
                value = lax.dot_general(
                    pick_ref[...], spread, NT_DIMS, preferred_element_type=jnp.float32
                )
                for c in range(band_local):
                    start = c * n_sta * sig_count + i * group * sig_count + sig
                    out_ref[pl.ds(start, group, stride=sig_count)] = value[
                        c * group : (c + 1) * group
                    ]
                return carry

            lax.fori_loop(0, n_groups, turn, 0)

        build_banded()
        coarse(0, True)
        for sig in range(sig_count):
            if sig + 1 < sig_count:
                coarse(sig + 1, False)
            fine(sig)
            post(sig)
        for sig in range(sig_count):
            collect(sig)
        for sig in range(sig_count):
            all_but_one(sig, send_sem.at[sig])

        @pl.when(my_win < n_win - 1)
        def _():
            for sig in range(sig_count):
                edge_copy(sig).wait_send()
                old_copy(sig).wait_send()

    dma = pltpu.SemaphoreType.DMA
    in_vmem = pl.BlockSpec(memory_space=pltpu.VMEM)
    bf16, f32 = jnp.bfloat16, jnp.float32
    return pl.pallas_call(
        kernel,
        out_shape=jax.ShapeDtypeStruct((band_local * n_sta * sig_count, 128), f32),
        in_specs=[in_vmem] * 6,
        out_specs=in_vmem,
        scratch_shapes=[
            pltpu.VMEM((cols, halo_rows + frame_count, 128), f32),
            pltpu.VMEM((sig_count, halo_rows, frame_len), bf16),
            pltpu.VMEM((sig_count, old_rows + fine_count * frame_rows, KEEP), bf16),
            pltpu.VMEM((fine_len * 2 * QUAD, span * frame_rows), bf16),
            pltpu.VMEM((n_quads, fine_len * 2 * QUAD, KEEP), f32),
            pltpu.VMEM((sig_count, n_all, 8, 128), bf16),
            pltpu.VMEM((sig_count, n_groups, n_win, 8, group * 128), bf16),
        ]
        + [dma((sig_count,))] * 7,
        compiler_params=pltpu.CompilerParams(
            collective_id=0, has_side_effects=True, vmem_limit_bytes=30 * 2**20
        ),
        name="channelise",
    )


def make_correlator(band_local, sig_all, scale):
    step = 4

    def kernel(x_ref, out_ref):
        part = lax.rem(lax.broadcasted_iota(jnp.int32, (sig_all, 128), 1), 8) < 4
        for c in range(step):
            x = x_ref[c]
            turned = jnp.where(part, pltpu.roll(x, 124, 1), -pltpu.roll(x, 4, 1))
            x = x.astype(jnp.bfloat16)
            turned = turned.astype(jnp.bfloat16)
            for index, left in enumerate((x, turned)):
                value = lax.dot_general(left, x, NT_DIMS, preferred_element_type=jnp.float32)
                out_ref[c, 0, index] = (value * scale).astype(jnp.bfloat16)

    return pl.pallas_call(
        kernel,
        grid=(band_local // step,),
        out_shape=jax.ShapeDtypeStruct((band_local, 1, 2, sig_all, sig_all), jnp.bfloat16),
        in_specs=[pl.BlockSpec((step, sig_all, 128), lambda i: (i, 0, 0))],
        out_specs=pl.BlockSpec((step, 1, 2, sig_all, sig_all), lambda i: (i, 0, 0, 0, 0)),
        compiler_params=pltpu.CompilerParams(vmem_limit_bytes=16 * 2**20),
        name="correlate",
    )


def per_device(samples, coarse_taps, fine_taps):
    n_win, n_sta = lax.axis_size("win"), lax.axis_size("sta")
    sig_local, samp_local = samples.shape
    tap_count, frame_len = coarse_taps.shape
    fine_tap_count, fine_len = fine_taps.shape
    frame_count = samp_local // frame_len
    band_local = KEEP // n_win
    frames = samples.reshape(sig_local, frame_count, frame_len)
    channelise = make_channeliser(
        n_win, n_sta, sig_local, frame_count, tap_count, frame_len, fine_tap_count, fine_len
    )
    fine = channelise(
        frames,
        coarse_taps,
        fine_taps,
        jnp.asarray(coarse_matrix(frame_len, KEEP)),
        jnp.asarray(fine_matrix(fine_len)),
        jnp.asarray(pick_matrix(band_local, 8, 128)),
    )
    frame_total = n_win * (frame_count // fine_len)
    correlate = make_correlator(band_local, n_sta * sig_local, 1.0 / frame_total)
    return correlate(fine.reshape(band_local, n_sta * sig_local, 128))


def solution(mesh):
    placed = (P("sta", "win"), P(), P())
    return jax.shard_map(
        per_device,
        mesh=mesh,
        in_specs=placed,
        out_specs=P("win", "sta", None, None, None),
        check_vma=False,
    )
```

time: 185 us -> 89.2 us (0.48)
  Pallas kernels: 0 us -> 85.9 us
  blocking collectives: 84.3 us -> 0 us
  local copies, waits for them, and re-layouts: 36.6 us -> 3.13 us
  other arithmetic: 28.6 us -> 0 us
  matrix products: 12.8 us -> 0 us
  starting transfers between devices: 11.8 us -> 0 us
  waiting for transfers between devices: 10.4 us -> 0 us
    pallas_call x0 -> x2, Pallas kernels: none -> 85.9 us  [the longest x1 79.7 us: per_device(): channelise(frames, coarse_taps, fine_taps, jnp.asarray(coarse_matrix(fram...]
    all_to_all x2 -> x0, blocking collectives: 84.3 us -> none  [the longest x1 52.7 us: per_device(): lax.all_to_all(local_spectra, 'sta', split_axis=1, concat_axis=2, tiled=T...]
    convert_element_type x4 -> x0, other arithmetic: 22 us -> none  [the longest x1 17.6 us: per_device(): windowed.astype(jnp.bfloat16).reshape(sig_local * frame_count, frame_len)]
    slice x3 -> x0, local copies, waits for them, and re-layouts: 15.1 us -> none  [the longest x1 15 us: per_device(): groups[:, start:start + fine_count].astype(jnp.float32)]
    dot_general x7 -> x0, matrix products: 12.8 us -> none  [the longest x1 2.31 us: per_device(): jnp.einsum('qj,sgjk->kqsg', cosines, imag_part, precision=highest)]
    ppermute x2 -> x0, starting transfers between devices: 11.8 us -> none  [from_behind(): return lax.ppermute(x, axis, pairs)]
    ppermute x2 -> x0, waiting for transfers between devices: 10.4 us -> none  [from_behind(): return lax.ppermute(x, axis, pairs)]
    convert_element_type x1 -> x0, local copies, waits for them, and re-layouts: 7.77 us -> none  [per_device(): return (vis_local / frame_total).astype(jnp.bfloat16)]
  transfers between devices with their start and end apart: 2 -> 0, of which waited for: 2 -> 0; matrix products, arithmetic and copies ran while one was open for 1% -> 0% of each run, Pallas kernels for 0% -> 0%
where the time goes in v2:
time: 89.2 us; the launch traced here: 89.1 us
  Pallas kernels  85.9 us (96%)
  local copies, waits for them, and re-layouts  3.13 us (4%)
    pallas_call x1, Pallas kernels, per_device(): channelise(frames, coarse_taps, fine_taps, jnp.asarray(coarse_matrix(fram...  79.7 us
    pallas_call x1, Pallas kernels, per_device(): return correlate(fine.reshape(band_local, n_sta * sig_local, 128))  6.26 us
    unnamed x11, local copies, waits for them, and re-layouts  3.13 us

profile of v2, /device:TPU:1, one launch (start us, length us, event | category | flops | bytes accessed | tf_op | source)
XLA Modules:
  0.0 89.1 jit_solution(11416805148050439294)
XLA Ops:
  0.0 0.0 copy-start
  0.0 0.0 copy-start.1
  0.0 0.0 copy-start.2
  0.0 0.0 copy-start.3
  0.0 0.0 copy-start.4
  0.0 3.1 %copy.9 = bf16[1,4,1024,512]{3,2,1,0:T(8,128)(2,1)S(1)} copy(bf16[1,4,1024,512]{3,1,2,0:T(4,128)(2,1)} %bitcast.7) | data formatting | bytes 8388608
  3.1 0.0 copy-done
  3.2 0.0 copy-done.1
  3.2 0.0 copy-done.2
  3.2 0.0 copy-done.3
  3.2 0.0 copy-done.4
  3.2 79.7 %channelise.1 = f32[8192,128]{1,0:T(8,128)S(1)} custom-call(bf16[4,1024,512]{2,1,0:T(8,128)(2,1)S(1)} %bitcast.6, bf16[16,512]{1,0:T(8,128)(2,1)S(1)} %copy-done.3, bf16[8,64]{1,0:T(8,128)(2,1)S(1)} %copy-done.4, bf16[512,256]{1,0:T(8,128)(2,1)S(1)} %copy-done.2, f32[512,128]{1,0:T(8,128)S(1)} %copy-done.1, bf16[256,1024]{1,0:T(8,128)(2,1)S(1)} %copy-done), custom_call_target="tpu_custom_call" | custom-call | tf_op jit(solution)/shard_map/channelise/pallas_call | solution.py:349
  82.9 6.3 %correlate.1 = bf16[32,1,2,256,256]{4,3,2,1,0:T(8,128)(2,1)} custom-call(f32[32,256,128]{2,1,0:T(8,128)S(1)} %bitcast.5), custom_call_target="tpu_custom_call" | custom-call | tf_op jit(solution)/shard_map/correlate/pallas_call | solution.py:359
Async XLA Ops:
  0.0 3.1 %copy-start = (bf16[256,1024]{1,0:T(8,128)(2,1)S(1)}, bf16[256,1024]{1,0:T(8,128)(2,1)}, u32[]{:S(2)}) copy-start(bf16[256,1024]{1,0:T(8,128)(2,1)} %constant.8.clone.pick_ref) | copy-start | bytes 1572868
  0.0 3.2 %copy-start.1 = (f32[512,128]{1,0:T(8,128)S(1)}, f32[512,128]{1,0:T(8,128)}, u32[]{:S(2)}) copy-start(f32[512,128]{1,0:T(8,128)} %constant.7.clone.table_ref) | copy-start | bytes 786436
  0.0 3.2 %copy-start.2 = (bf16[512,256]{1,0:T(8,128)(2,1)S(1)}, bf16[512,256]{1,0:T(8,128)(2,1)}, u32[]{:S(2)}) copy-start(bf16[512,256]{1,0:T(8,128)(2,1)} %constant.6.clone.dft_ref) | copy-start | bytes 786436
  0.0 3.2 %copy-start.3 = (bf16[16,512]{1,0:T(8,128)(2,1)S(1)}, bf16[16,512]{1,0:T(8,128)(2,1)}, u32[]{:S(2)}) copy-start(bf16[16,512]{1,0:T(8,128)(2,1)} %coarse_ref.1) | copy-start | bytes 49156
  0.0 3.2 %copy-start.4 = (bf16[8,64]{1,0:T(8,128)(2,1)S(1)}, bf16[8,64]{1,0:T(8,128)(2,1)}, u32[]{:S(2)}) copy-start(bf16[8,64]{1,0:T(8,128)(2,1)} %fine_ref.1) | copy-start | bytes 3076

commit v3 on v2

--- a/solution.py
+++ b/solution.py
@@ -53,11 +53,12 @@
     band_local = KEEP // n_win
     group = 8
     n_groups = n_sta // group
+    n_row = 16
 
     def kernel(
         x_ref, coarse_ref, fine_ref, dft_ref, table_ref, pick_ref, out_ref,
         wide, edge, spec, banded, stage, outbox, inbox,
-        own_sem, edge_send, edge_recv, old_send, old_recv, send_sem, recv_sem,
+        met, own_sem, edge_send, edge_recv, old_send, old_recv, send_sem, recv_sem,
     ):
         my_win = lax.axis_index("win")
         my_sta = lax.axis_index("sta")
@@ -68,11 +69,32 @@
             sta = lax.rem(my_sta + lax.rem(step, n_sta), n_sta)
             return win, sta
 
-        def greet(step, carry):
-            pl.semaphore_signal(barrier, inc=1, device_id=peer(step), device_id_type=MESH_ID)
+        n_col = n_all // n_row
+        sta_rows = n_sta // n_row
+        my_col = my_win * sta_rows + my_sta // n_row
+        my_row = lax.rem(my_sta, n_row)
+
+        def along_row(step):
+            return my_win, my_sta - my_row + lax.rem(my_row + step, n_row)
+
+        def along_col(step):
+            col = lax.rem(my_col + step, n_col)
+            return col // sta_rows, lax.rem(col, sta_rows) * n_row + my_row
+
+        def greet_row(step, carry):
+            pl.semaphore_signal(barrier, inc=1, device_id=along_row(step), device_id_type=MESH_ID)
             return carry
 
-        lax.fori_loop(1, n_all, greet, 0)
+        def greet_col(step, carry):
+            pl.semaphore_signal(barrier, inc=1, device_id=along_col(step), device_id_type=MESH_ID)
+            return carry
+
+        def pass_on(step, carry):
+            pl.semaphore_signal(met, inc=1, device_id=along_col(step), device_id_type=MESH_ID)
+            return carry
+
+        lax.fori_loop(1, n_row, greet_row, 0)
+        lax.fori_loop(1, n_col, greet_col, 0)
 
         def edge_copy(sig):
             return pltpu.make_async_remote_copy(
@@ -142,7 +164,7 @@
 
             lax.fori_loop(n_blocks // 2, n_blocks, step, 0)
             if first:
-                pl.semaphore_wait(barrier, n_all - 1)
+                pl.semaphore_wait(met, n_col - 1)
 
                 @pl.when(my_win < n_win - 1)
                 def _():
@@ -178,12 +200,18 @@
             def _():
                 old_copy(sig).wait_recv()
 
-            for quad in range(n_quads):
-                stage[quad] = jnp.dot(
+            for quad in range(0, n_quads, 2):
+                windows = [
+                    spec[sig, pl.ds(q * QUAD * frame_rows, span * frame_rows)]
+                    for q in (quad, quad + 1)
+                ]
+                result = jnp.dot(
                     banded[...],
-                    spec[sig, pl.ds(quad * QUAD * frame_rows, span * frame_rows)],
+                    jnp.concatenate(windows, axis=1),
                     preferred_element_type=jnp.float32,
                 )
+                stage[quad] = result[:, :KEEP]
+                stage[quad + 1] = result[:, KEEP:]
 
             def turn(i, carry):
                 rows = pl.ds(pl.multiple_of(i * 64, 64), 64)
@@ -222,19 +250,23 @@
             ]
             pltpu.make_async_copy(outbox.at[sig, my_win * n_sta + my_sta], mine, own_sem.at[sig]).start()
 
-            def send(step, carry):
-                win, sta = peer(step)
-                pltpu.make_async_remote_copy(
-                    src_ref=outbox.at[sig, win * n_sta + sta],
-                    dst_ref=mine,
-                    send_sem=send_sem.at[sig],
-                    recv_sem=recv_sem.at[sig],
-                    device_id=(win, sta),
-                    device_id_type=MESH_ID,
-                ).start()
-                return carry
-
-            lax.fori_loop(1, n_all, send, 0)
+            for turn in range(n_win):
+                win = lax.rem(my_win + turn, n_win)
+                first = 1 if turn == 0 else 0
+
+                def send(step, carry, win=win):
+                    sta = lax.rem(my_sta + step, n_sta)
+                    pltpu.make_async_remote_copy(
+                        src_ref=outbox.at[sig, win * n_sta + sta],
+                        dst_ref=mine,
+                        send_sem=send_sem.at[sig],
+                        recv_sem=recv_sem.at[sig],
+                        device_id=(win, sta),
+                        device_id_type=MESH_ID,
+                    ).start()
+                    return carry
+
+                lax.fori_loop(first, n_sta, send, 0, unroll=7 if first else 8)
 
         def all_but_one(sig, sem):
             most = outbox.at[sig, pl.ds(0, n_all - 1)]
@@ -247,29 +279,36 @@
             which = lax.rem(lax.broadcasted_iota(jnp.int32, (8 * n_win, group * 128), 1), 128) // 32
 
             def turn(i, carry):
-                got = inbox[sig, i].astype(jnp.float32).reshape(n_win * 8, group * 128)
-                spread = jnp.concatenate(
-                    [
-                        jnp.where(which == quad, got, 0.0).astype(jnp.bfloat16)
-                        for quad in range(n_quads)
-                    ],
-                    axis=0,
-                )
+                spread = []
+                for half in range(2):
+                    got = inbox[sig, 2 * i + half].astype(jnp.float32)
+                    got = got.reshape(n_win * 8, group * 128)
+                    for quad in range(n_quads):
+                        spread.append(jnp.where(which == quad, got, 0.0).astype(jnp.bfloat16))
                 value = lax.dot_general(
-                    pick_ref[...], spread, NT_DIMS, preferred_element_type=jnp.float32
-                )
-                for c in range(band_local):
-                    start = c * n_sta * sig_count + i * group * sig_count + sig
-                    out_ref[pl.ds(start, group, stride=sig_count)] = value[
-                        c * group : (c + 1) * group
-                    ]
+                    pick_ref[...],
+                    jnp.concatenate(spread, axis=0),
+                    NT_DIMS,
+                    preferred_element_type=jnp.float32,
+                )
+                for half in range(2):
+                    for c in range(band_local):
+                        start = c * n_sta * sig_count + (2 * i + half) * group * sig_count + sig
+                        out_ref[pl.ds(start, group, stride=sig_count)] = value[
+                            c * group : (c + 1) * group, half * 128 : (half + 1) * 128
+                        ]
                 return carry
 
-            lax.fori_loop(0, n_groups, turn, 0)
+            lax.fori_loop(0, n_groups // 2, turn, 0)
 
         build_banded()
+        pl.semaphore_wait(barrier, n_row + n_col - 2)
+        lax.fori_loop(1, n_col, pass_on, 0)
         coarse(0, True)
-        for sig in range(sig_count):
+        fine(0)
+        post(0)
+        coarse(1, False)
+        for sig in range(1, sig_count):
             if sig + 1 < sig_count:
                 coarse(sig + 1, False)
             fine(sig)
@@ -302,6 +341,7 @@
             pltpu.VMEM((sig_count, n_all, 8, 128), bf16),
             pltpu.VMEM((sig_count, n_groups, n_win, 8, group * 128), bf16),
         ]
+        + [pltpu.SemaphoreType.REGULAR]
         + [dma((sig_count,))] * 7,
         compiler_params=pltpu.CompilerParams(
             collective_id=0, has_side_effects=True, vmem_limit_bytes=30 * 2**20
@@ -312,24 +352,49 @@
 
 def make_correlator(band_local, sig_all, scale):
     step = 4
-
-    def kernel(x_ref, out_ref):
+    slots = 2
+    n_steps = band_local // step
+
+    def kernel(x_ref, out_ref, held, sems):
         part = lax.rem(lax.broadcasted_iota(jnp.int32, (sig_all, 128), 1), 8) < 4
-        for c in range(step):
-            x = x_ref[c]
-            turned = jnp.where(part, pltpu.roll(x, 124, 1), -pltpu.roll(x, 4, 1))
-            x = x.astype(jnp.bfloat16)
-            turned = turned.astype(jnp.bfloat16)
-            for index, left in enumerate((x, turned)):
-                value = lax.dot_general(left, x, NT_DIMS, preferred_element_type=jnp.float32)
-                out_ref[c, 0, index] = (value * scale).astype(jnp.bfloat16)
+
+        def put(i, slot):
+            return pltpu.make_async_copy(
+                held.at[slot], out_ref.at[pl.ds(i * step, step)], sems.at[slot]
+            )
+
+        def work(i, carry):
+            slot = lax.rem(i, slots)
+
+            @pl.when(i >= slots)
+            def _():
+                put(i - slots, slot).wait()
+
+            for c in range(step):
+                x = x_ref[i * step + c]
+                turned = jnp.where(part, pltpu.roll(x, 124, 1), -pltpu.roll(x, 4, 1))
+                x = x.astype(jnp.bfloat16)
+                both = jnp.concatenate([x, turned.astype(jnp.bfloat16)], axis=0)
+                value = lax.dot_general(both, x, NT_DIMS, preferred_element_type=jnp.float32)
+                value = (value * scale).astype(jnp.bfloat16)
+                held[slot, c, 0, 0] = value[:sig_all]
+                held[slot, c, 0, 1] = value[sig_all:]
+            put(i, slot).start()
+            return carry
+
+        lax.fori_loop(0, n_steps, work, 0)
+        for i in range(n_steps - slots, n_steps):
+            put(i, i % slots).wait()
 
     return pl.pallas_call(
         kernel,
-        grid=(band_local // step,),
         out_shape=jax.ShapeDtypeStruct((band_local, 1, 2, sig_all, sig_all), jnp.bfloat16),
-        in_specs=[pl.BlockSpec((step, sig_all, 128), lambda i: (i, 0, 0))],
-        out_specs=pl.BlockSpec((step, 1, 2, sig_all, sig_all), lambda i: (i, 0, 0, 0, 0)),
+        in_specs=[pl.BlockSpec(memory_space=pltpu.VMEM)],
+        out_specs=pl.BlockSpec(memory_space=pl.ANY),
+        scratch_shapes=[
+            pltpu.VMEM((slots, step, 1, 2, sig_all, sig_all), jnp.bfloat16),
+            pltpu.SemaphoreType.DMA((slots,)),
+        ],
         compiler_params=pltpu.CompilerParams(vmem_limit_bytes=16 * 2**20),
         name="correlate",
     )

time: 89.2 us -> 80.3 us (0.900)
  Pallas kernels: 85.9 us -> 77.1 us
    pallas_call x1, Pallas kernels: 79.7 us -> 70.9 us  [per_device(): channelise(frames, coarse_taps, fine_taps, jnp.asarray(coarse_matrix(fram...]
where the time goes in v3:
time: 80.3 us
  Pallas kernels  77.1 us (96%)
  local copies, waits for them, and re-layouts  3.13 us (4%)
    pallas_call x1, Pallas kernels, per_device(): channelise(frames, coarse_taps, fine_taps, jnp.asarray(coarse_matrix(fram...  70.9 us
    pallas_call x1, Pallas kernels, per_device(): return correlate(fine.reshape(band_local, n_sta * sig_local, 128))  6.17 us
    unnamed x11, local copies, waits for them, and re-layouts  3.13 us

profile of v3, /device:TPU:1, one launch (start us, length us, event | category | flops | bytes accessed | tf_op | source)
XLA Modules:
  0.0 80.3 jit_solution(8130243270939690970)
XLA Ops:
  0.0 0.0 copy-start
  0.0 0.0 copy-start.1
  0.0 0.0 copy-start.2
  0.0 0.0 copy-start.3
  0.0 0.0 copy-start.4
  0.0 3.1 %copy.9 = bf16[1,4,1024,512]{3,2,1,0:T(8,128)(2,1)S(1)} copy(bf16[1,4,1024,512]{3,1,2,0:T(4,128)(2,1)} %bitcast.7) | data formatting | bytes 8388608
  3.1 0.0 copy-done
  3.2 0.0 copy-done.1
  3.2 0.0 copy-done.2
  3.2 0.0 copy-done.3
  3.2 0.0 copy-done.4
  3.2 70.9 %channelise.1 = f32[8192,128]{1,0:T(8,128)S(1)} custom-call(bf16[4,1024,512]{2,1,0:T(8,128)(2,1)S(1)} %bitcast.6, bf16[16,512]{1,0:T(8,128)(2,1)S(1)} %copy-done.3, bf16[8,64]{1,0:T(8,128)(2,1)S(1)} %copy-done.4, bf16[512,256]{1,0:T(8,128)(2,1)S(1)} %copy-done.2, f32[512,128]{1,0:T(8,128)S(1)} %copy-done.1, bf16[256,1024]{1,0:T(8,128)(2,1)S(1)} %copy-done), custom_call_target="tpu_custom_call" | custom-call | tf_op jit(solution)/shard_map/channelise/pallas_call | solution.py:414
  74.1 6.2 %correlate.1 = bf16[32,1,2,256,256]{4,3,2,1,0:T(8,128)(2,1)} custom-call(f32[32,256,128]{2,1,0:T(8,128)S(1)} %bitcast.5), custom_call_target="tpu_custom_call" | custom-call | tf_op jit(solution)/shard_map/correlate/pallas_call | solution.py:424
Async XLA Ops:
  0.0 3.1 %copy-start = (bf16[256,1024]{1,0:T(8,128)(2,1)S(1)}, bf16[256,1024]{1,0:T(8,128)(2,1)}, u32[]{:S(2)}) copy-start(bf16[256,1024]{1,0:T(8,128)(2,1)} %constant.8.clone.pick_ref) | copy-start | bytes 1572868
  0.0 3.2 %copy-start.1 = (f32[512,128]{1,0:T(8,128)S(1)}, f32[512,128]{1,0:T(8,128)}, u32[]{:S(2)}) copy-start(f32[512,128]{1,0:T(8,128)} %constant.7.clone.table_ref) | copy-start | bytes 786436
  0.0 3.2 %copy-start.2 = (bf16[512,256]{1,0:T(8,128)(2,1)S(1)}, bf16[512,256]{1,0:T(8,128)(2,1)}, u32[]{:S(2)}) copy-start(bf16[512,256]{1,0:T(8,128)(2,1)} %constant.6.clone.dft_ref) | copy-start | bytes 786436
  0.0 3.2 %copy-start.3 = (bf16[16,512]{1,0:T(8,128)(2,1)S(1)}, bf16[16,512]{1,0:T(8,128)(2,1)}, u32[]{:S(2)}) copy-start(bf16[16,512]{1,0:T(8,128)(2,1)} %coarse_ref.1) | copy-start | bytes 49156
  0.0 3.2 %copy-start.4 = (bf16[8,64]{1,0:T(8,128)(2,1)S(1)}, bf16[8,64]{1,0:T(8,128)(2,1)}, u32[]{:S(2)}) copy-start(bf16[8,64]{1,0:T(8,128)(2,1)} %fine_ref.1) | copy-start | bytes 3076

commit v4 on v3

--- a/solution.py
+++ b/solution.py
@@ -164,16 +164,17 @@
 
             lax.fori_loop(n_blocks // 2, n_blocks, step, 0)
             if first:
-                pl.semaphore_wait(met, n_col - 1)
-
-                @pl.when(my_win < n_win - 1)
-                def _():
-                    for s in range(sig_count):
-                        edge_copy(s).start()
+                pl.semaphore_wait(barrier, n_row + n_col - 2)
+                lax.fori_loop(1, n_col, pass_on, 0)
 
             @pl.when(my_win < n_win - 1)
             def _():
+                if first:
+                    edge_copy(0).start()
                 old_copy(sig).start()
+                if first:
+                    for s in range(1, sig_count):
+                        edge_copy(s).start()
 
             lax.fori_loop(1, n_blocks // 2, step, 0)
 
@@ -302,10 +303,9 @@
             lax.fori_loop(0, n_groups // 2, turn, 0)
 
         build_banded()
-        pl.semaphore_wait(barrier, n_row + n_col - 2)
-        lax.fori_loop(1, n_col, pass_on, 0)
         coarse(0, True)
         fine(0)
+        pl.semaphore_wait(met, n_col - 1)
         post(0)
         coarse(1, False)
         for sig in range(1, sig_count):
@@ -352,7 +352,7 @@
 
 def make_correlator(band_local, sig_all, scale):
     step = 4
-    slots = 2
+    slots = 4
     n_steps = band_local // step
 
     def kernel(x_ref, out_ref, held, sems):

time: 80.3 us -> 75.4 us (0.939)
  Pallas kernels: 77.1 us -> 72.2 us
    pallas_call x1, Pallas kernels: 70.9 us -> 67.5 us  [per_device(): channelise(frames, coarse_taps, fine_taps, jnp.asarray(coarse_matrix(fram...]
    pallas_call x1, Pallas kernels: 6.17 us -> 4.66 us  [per_device(): return correlate(fine.reshape(band_local, n_sta * sig_local, 128))]
where the time goes in v4:
time: 75.4 us
  Pallas kernels  72.2 us (96%)
  local copies, waits for them, and re-layouts  3.13 us (4%)
    pallas_call x1, Pallas kernels, per_device(): channelise(frames, coarse_taps, fine_taps, jnp.asarray(coarse_matrix(fram...  67.5 us
    pallas_call x1, Pallas kernels, per_device(): return correlate(fine.reshape(band_local, n_sta * sig_local, 128))  4.66 us
    unnamed x11, local copies, waits for them, and re-layouts  3.13 us

profile of v4, /device:TPU:1, one launch (start us, length us, event | category | flops | bytes accessed | tf_op | source)
XLA Modules:
  0.0 75.4 jit_solution(15925699115515482001)
XLA Ops:
  0.0 0.0 copy-start
  0.0 0.0 copy-start.1
  0.0 0.0 copy-start.2
  0.0 0.0 copy-start.3
  0.0 0.0 copy-start.4
  0.0 3.1 %copy.9 = bf16[1,4,1024,512]{3,2,1,0:T(8,128)(2,1)S(1)} copy(bf16[1,4,1024,512]{3,1,2,0:T(4,128)(2,1)} %bitcast.7) | data formatting | bytes 8388608
  3.1 0.0 copy-done
  3.2 0.0 copy-done.1
  3.2 0.0 copy-done.2
  3.2 0.0 copy-done.3
  3.2 0.0 copy-done.4
  3.2 67.5 %channelise.1 = f32[8192,128]{1,0:T(8,128)S(1)} custom-call(bf16[4,1024,512]{2,1,0:T(8,128)(2,1)S(1)} %bitcast.6, bf16[16,512]{1,0:T(8,128)(2,1)S(1)} %copy-done.3, bf16[8,64]{1,0:T(8,128)(2,1)S(1)} %copy-done.4, bf16[512,256]{1,0:T(8,128)(2,1)S(1)} %copy-done.2, f32[512,128]{1,0:T(8,128)S(1)} %copy-done.1, bf16[256,1024]{1,0:T(8,128)(2,1)S(1)} %copy-done), custom_call_target="tpu_custom_call" | custom-call | tf_op jit(solution)/shard_map/channelise/pallas_call | solution.py:414
  70.7 4.7 %correlate.1 = bf16[32,1,2,256,256]{4,3,2,1,0:T(8,128)(2,1)} custom-call(f32[32,256,128]{2,1,0:T(8,128)S(1)} %bitcast.5), custom_call_target="tpu_custom_call" | custom-call | tf_op jit(solution)/shard_map/correlate/pallas_call | solution.py:424
Async XLA Ops:
  0.0 3.1 %copy-start = (bf16[256,1024]{1,0:T(8,128)(2,1)S(1)}, bf16[256,1024]{1,0:T(8,128)(2,1)}, u32[]{:S(2)}) copy-start(bf16[256,1024]{1,0:T(8,128)(2,1)} %constant.8.clone.pick_ref) | copy-start | bytes 1572868
  0.0 3.2 %copy-start.1 = (f32[512,128]{1,0:T(8,128)S(1)}, f32[512,128]{1,0:T(8,128)}, u32[]{:S(2)}) copy-start(f32[512,128]{1,0:T(8,128)} %constant.7.clone.table_ref) | copy-start | bytes 786436
  0.0 3.2 %copy-start.2 = (bf16[512,256]{1,0:T(8,128)(2,1)S(1)}, bf16[512,256]{1,0:T(8,128)(2,1)}, u32[]{:S(2)}) copy-start(bf16[512,256]{1,0:T(8,128)(2,1)} %constant.6.clone.dft_ref) | copy-start | bytes 786436
  0.0 3.2 %copy-start.3 = (bf16[16,512]{1,0:T(8,128)(2,1)S(1)}, bf16[16,512]{1,0:T(8,128)(2,1)}, u32[]{:S(2)}) copy-start(bf16[16,512]{1,0:T(8,128)(2,1)} %coarse_ref.1) | copy-start | bytes 49156
  0.0 3.2 %copy-start.4 = (bf16[8,64]{1,0:T(8,128)(2,1)S(1)}, bf16[8,64]{1,0:T(8,128)(2,1)}, u32[]{:S(2)}) copy-start(bf16[8,64]{1,0:T(8,128)(2,1)} %fine_ref.1) | copy-start | bytes 3076

commit v5 on v4

--- a/solution.py
+++ b/solution.py
@@ -302,8 +302,8 @@
 
             lax.fori_loop(0, n_groups // 2, turn, 0)
 
+        coarse(0, True)
         build_banded()
-        coarse(0, True)
         fine(0)
         pl.semaphore_wait(met, n_col - 1)
         post(0)

time: 75.4 us -> 75.3 us (level)
  no operation moved by 1% of the time
where the time goes in v5:
time: 75.3 us; the launch traced here: 75.2 us
  Pallas kernels  72 us (96%)
  local copies, waits for them, and re-layouts  3.13 us (4%)
    pallas_call x1, Pallas kernels, per_device(): channelise(frames, coarse_taps, fine_taps, jnp.asarray(coarse_matrix(fram...  67.4 us
    pallas_call x1, Pallas kernels, per_device(): return correlate(fine.reshape(band_local, n_sta * sig_local, 128))  4.66 us
    unnamed x11, local copies, waits for them, and re-layouts  3.13 us

profile of v5, /device:TPU:1, one launch (start us, length us, event | category | flops | bytes accessed | tf_op | source)
XLA Modules:
  0.0 75.2 jit_solution(15690919433675823597)
XLA Ops:
  0.0 0.0 copy-start
  0.0 0.0 copy-start.1
  0.0 0.0 copy-start.2
  0.0 0.0 copy-start.3
  0.0 0.0 copy-start.4
  0.0 3.1 %copy.9 = bf16[1,4,1024,512]{3,2,1,0:T(8,128)(2,1)S(1)} copy(bf16[1,4,1024,512]{3,1,2,0:T(4,128)(2,1)} %bitcast.7) | data formatting | bytes 8388608
  3.1 0.0 copy-done
  3.2 0.0 copy-done.1
  3.2 0.0 copy-done.2
  3.2 0.0 copy-done.3
  3.2 0.0 copy-done.4
  3.2 67.4 %channelise.1 = f32[8192,128]{1,0:T(8,128)S(1)} custom-call(bf16[4,1024,512]{2,1,0:T(8,128)(2,1)S(1)} %bitcast.6, bf16[16,512]{1,0:T(8,128)(2,1)S(1)} %copy-done.3, bf16[8,64]{1,0:T(8,128)(2,1)S(1)} %copy-done.4, bf16[512,256]{1,0:T(8,128)(2,1)S(1)} %copy-done.2, f32[512,128]{1,0:T(8,128)S(1)} %copy-done.1, bf16[256,1024]{1,0:T(8,128)(2,1)S(1)} %copy-done), custom_call_target="tpu_custom_call" | custom-call | tf_op jit(solution)/shard_map/channelise/pallas_call | solution.py:414
  70.6 4.7 %correlate.1 = bf16[32,1,2,256,256]{4,3,2,1,0:T(8,128)(2,1)} custom-call(f32[32,256,128]{2,1,0:T(8,128)S(1)} %bitcast.5), custom_call_target="tpu_custom_call" | custom-call | tf_op jit(solution)/shard_map/correlate/pallas_call | solution.py:424
Async XLA Ops:
  0.0 3.1 %copy-start = (bf16[256,1024]{1,0:T(8,128)(2,1)S(1)}, bf16[256,1024]{1,0:T(8,128)(2,1)}, u32[]{:S(2)}) copy-start(bf16[256,1024]{1,0:T(8,128)(2,1)} %constant.8.clone.pick_ref) | copy-start | bytes 1572868
  0.0 3.2 %copy-start.1 = (f32[512,128]{1,0:T(8,128)S(1)}, f32[512,128]{1,0:T(8,128)}, u32[]{:S(2)}) copy-start(f32[512,128]{1,0:T(8,128)} %constant.7.clone.table_ref) | copy-start | bytes 786436
  0.0 3.2 %copy-start.2 = (bf16[512,256]{1,0:T(8,128)(2,1)S(1)}, bf16[512,256]{1,0:T(8,128)(2,1)}, u32[]{:S(2)}) copy-start(bf16[512,256]{1,0:T(8,128)(2,1)} %constant.6.clone.dft_ref) | copy-start | bytes 786436
  0.0 3.2 %copy-start.3 = (bf16[16,512]{1,0:T(8,128)(2,1)S(1)}, bf16[16,512]{1,0:T(8,128)(2,1)}, u32[]{:S(2)}) copy-start(bf16[16,512]{1,0:T(8,128)(2,1)} %coarse_ref.1) | copy-start | bytes 49156
  0.0 3.2 %copy-start.4 = (bf16[8,64]{1,0:T(8,128)(2,1)S(1)}, bf16[8,64]{1,0:T(8,128)(2,1)}, u32[]{:S(2)}) copy-start(bf16[8,64]{1,0:T(8,128)(2,1)} %fine_ref.1) | copy-start | bytes 3076
